TPU v7x, 64 devices: a 2x2x8 block of a 4x4x8 slice. The times are simulated.
64 devices in a mesh: rep: 4 (over x, y), dp: 16 (over z, core).
Axes of the slice: x: 2, y: 2, z: 8, core: 2. Of those that a mesh axis runs over, the one named last changes fastest.
The devices are a block of a 4x4x8 slice.
Arguments:
- x: bfloat16 [64, 2048, 512], P(('rep', 'dp')), parts along dimension 0
- dy: bfloat16 [64, 2048, 512], P(('rep', 'dp')), parts along dimension 0
- w_gate: bfloat16 [2, 512, 1280], replicated
- w_up: bfloat16 [2, 512, 1280], replicated
- w_down: bfloat16 [2, 1280, 512], replicated
- m_w_gate: float32 [2, 512, 1280], P(None, 'dp')
- m_w_up: float32 [2, 512, 1280], P(None, 'dp')
- m_w_down: float32 [2, 1280, 512], P(None, 'dp')
- v_w_gate: float32 [2, 512, 1280], P(None, 'dp')
- v_w_up: float32 [2, 512, 1280], P(None, 'dp')
- v_w_down: float32 [2, 1280, 512], P(None, 'dp')
Outputs:
- output 1: bfloat16 [8, 512, 1280], P('rep'), parts along dimension 0
- output 2: bfloat16 [8, 512, 1280], P('rep'), parts along dimension 0
- output 3: bfloat16 [8, 1280, 512], P('rep'), parts along dimension 0
- output 4: float32 [8, 512, 1280], P('rep', 'dp'), parts along dimension 0
- output 5: float32 [8, 512, 1280], P('rep', 'dp'), parts along dimension 0
- output 6: float32 [8, 1280, 512], P('rep', 'dp'), parts along dimension 0
- output 7: float32 [8, 512, 1280], P('rep', 'dp'), parts along dimension 0
- output 8: float32 [8, 512, 1280], P('rep', 'dp'), parts along dimension 0
- output 9: float32 [8, 1280, 512], P('rep', 'dp'), parts along dimension 0
There are 4 independent parts. A program takes and returns all parts, laid end to end along the dimension named above; an argument that names none is the same for every part.
All inputs are finite; a program needn't handle non-finite values.
Results may differ from a plain program's by a relative error of at most 0.022.
Values are sent between devices in bfloat16 or wider.
A program may use at most 768 MiB of HBM per device.

v0:
```python
import jax
import jax.numpy as jnp
from jax import lax

NAMES = ("w_gate", "w_up", "w_down")


def matmul(a, w):
    return jnp.dot(a, w, preferred_element_type=jnp.float32).astype(jnp.bfloat16)


def normed(h):
    wide = h.astype(jnp.float32)
    scale = lax.rsqrt(jnp.mean(wide**2, -1, keepdims=True) + 1e-6)
    return (wide * scale).astype(jnp.bfloat16)


def layer(h, w):
    a = normed(h)
    gate = jnp.dot(a, w["w_gate"], preferred_element_type=jnp.float32)
    up = jnp.dot(a, w["w_up"], preferred_element_type=jnp.float32)
    return h + matmul((jax.nn.silu(gate) * up).astype(jnp.bfloat16), w["w_down"])


def adamw(w, m, v, g):
    m = 0.9 * m + 0.1 * g
    v = 0.95 * v + 0.05 * g * g
    step = m * lax.rsqrt(v + 1e-8) + 0.1 * w
    return (w - 0.02 * step).astype(jnp.bfloat16), m, v


def clipped(gradients, sum_of_squares, count):
    factor = jnp.minimum(1.0, 0.5 * lax.rsqrt(sum_of_squares / count + 1e-30))
    return [g * factor for g in gradients]


def stack(weights, h):
    for number in range(weights["w_gate"].shape[0]):
        h = layer(h, {name: w[number] for name, w in weights.items()})
    return h


def solution(mesh):
    groups = mesh.shape["rep"]

    def step(x, dy, *arrays):
        weights, m, v = (arrays[i : i + 3] for i in (0, 3, 6))
        x, dy = (t.reshape(groups, -1, *t.shape[1:]) for t in (x, dy))

        def of_a_group(x, dy):
            _, back = jax.vjp(lambda w: stack(w, x), dict(zip(NAMES, weights, strict=True)))
            by_weights = back(dy)[0]
            gradients = [by_weights[name].astype(jnp.float32) for name in NAMES]
            gradients = clipped(gradients, sum(jnp.sum(g * g) for g in gradients), sum(g.size for g in gradients))
            new = [adamw(w.astype(jnp.float32), m, v, g) for w, m, v, g in zip(weights, m, v, gradients, strict=True)]
            return tuple(one[which] for which in range(3) for one in new)

        return tuple(t.reshape(-1, *t.shape[2:]) for t in jax.vmap(of_a_group)(x, dy))

    return step
```

profile of v0, /device:TPU:21, one launch (start us, length us, event | category | flops | bytes accessed | tf_op | source)
XLA Modules:
  0.0 746.3 jit_solution(13730574523005766504)
XLA Ops:
  15.8 7.4 fusion.160
  26.2 7.9 %fusion.156 = (bf16[1,1,2048,1280]{3,2,1,0:T(8,128)(2,1)}, f32[2048,1280]{1,0:T(8,128)}) fusion(f32[2048,1280]{1,0:T(8,128)S(1)} %fusion.209, bf16[2,512,1280]{2,1,0:T(8,128)(2,1)S(1)} %copy-done.24, bf16[1,2048,512]{2,1,0:T(8,128)(2,1)S(1)} %copy-done.7, f32[2048]{0:T(1024)S(1)} %add_rsqrt_fusion), kind=kOutput, calls=%fused_computation.191 | convolution fusion | flops 2703228928 | bytes 29630464 | tf_op jit(solution)/vmap(jvp())/dot_general | solution.py:21
  34.8 8.1 %copy.4 = bf16[1,1,2048,1280]{2,3,1,0:T(8,128)(2,1)} copy(bf16[1,1,2048,1280]{3,2,1,0:T(8,128)(2,1)} %get-tuple-element.263) | data formatting | bytes 10485760
  42.9 6.1 fusion.168
  51.5 5.7 fusion.197
  57.2 13.1 %fusion.145 = (bf16[1,1,2048,1280]{3,2,1,0:T(8,128)(2,1)S(1)}, bf16[1,1,2048,1280]{3,2,1,0:T(8,128)(2,1)S(1)}, f32[2048,1280]{1,0:T(8,128)}) fusion(f32[2048,1280]{1,0:T(8,128)} %fusion.197, bf16[1,1,2048,1280]{3,2,1,0:T(8,128)(2,1)} %fusion.160, bf16[2,512,1280]{2,1,0:T(8,128)(2,1)} %param.12, bf16[1,1,2048,512]{2,3,1,0:T(8,128)(2,1)S(1)} %fusion.169), kind=kOutput, calls=%fused_computation.175 | convolution fusion | flops 2723676160 | bytes 40108032 | tf_op jit(solution)/vmap(jvp())/dot_general | solution.py:20
  70.4 5.6 fusion.174
  86.9 63.6 %while.17 = (bf16[1,1,2048,1280]{2,3,1,0:T(8,128)(2,1)}, bf16[1,1,2048,512]{3,2,1,0:T(8,128)(2,1)}, f32[1,80,512]{2,1,0:T(8,128)S(1)}, f32[1,80,512]{2,1,0:T(8,1...) while((bf16[1,1,2048,1280]{2,3,1,0:T(8,128)(2,1)}, ...), condition=%wide.windowed_dot_general_cond_rs.5.clone, body=%wide.windowed_dot_general_body_rs.5.clone.sunk | while | flops 673955840 | bytes 49939100 | solution.py:9
  103.5 4.6 collective-permute-start.21
  119.8 4.1 collective-permute-start.21
  135.6 4.1 collective-permute-start.21
  150.4 10.8 %fusion.155 = bf16[1,1,2048,1280]{3,2,1,0:T(8,128)(2,1)} fusion(f32[2048,1280]{1,0:T(8,128)} %fusion.197, f32[2048,1280]{1,0:T(8,128)} %get-tuple-element.267), kind=kLoop, calls=%fused_computation.189 | loop fusion | flops 15728640 | bytes 26214400 | tf_op jit(solution)/vmap(jvp())/convert_element_type | solution.py:22
  161.3 8.0 %copy.2 = bf16[1,1,2048,1280]{2,3,1,0:T(8,128)(2,1)} copy(bf16[1,1,2048,1280]{3,2,1,0:T(8,128)(2,1)} %fusion.155) | data formatting | bytes 10485760
  173.3 62.4 %while.16 = (bf16[1,1,2048,1280]{2,3,1,0:T(8,128)(2,1)}, bf16[1,1,2048,512]{3,2,1,0:T(8,128)(2,1)}, f32[1,80,512]{2,1,0:T(8,128)S(1)}, f32[1,80,512]{2,1,0:T(8,1...) while((bf16[1,1,2048,1280]{2,3,1,0:T(8,128)(2,1)}, ...), condition=%wide.windowed_dot_general_cond_rs.4.clone, body=%wide.windowed_dot_general_body_rs.4.clone.sunk | while | flops 673955840 | bytes 49939100 | solution.py:9
  205.1 4.1 collective-permute-start.17
  239.2 15.5 %convert_multiply_fusion = (bf16[1,1,2048,1280]{3,2,1,0:T(8,128)(2,1)}, bf16[1,1,2048,1280]{3,2,1,0:T(8,128)(2,1)}) fusion(f32[2048,1280]{1,0:T(8,128)} %copy-done.29, f32[2048,1280]{1,0:T(8,128)} %get-tuple-element.264, bf16[2,1280,512]{2,1,0:T(8,128)(2,1)} %param.16, bf16[1,1,2048,512]{2,3,1,0:T(8,128)(2,1)} %fusion.192), kind=kOutput, calls=%fused_computation.170 | convolution fusion | flops 2726297600 | bytes 34865152 | tf_op jit(solution)/vmap(transpose(jvp()))/dot_general | solution.py:9
  254.7 70.8 %while.15 = (bf16[1,1,2048,512]{2,3,1,0:T(8,128)(2,1)}, bf16[1,1,2048,1280]{3,2,1,0:T(8,128)(2,1)}, f32[1,32,1280]{2,1,0:T(8,128)S(1)}, f32[1,32,1280]{2,1,0:T(8...) while((bf16[1,1,2048,512]{2,3,1,0:T(8,128)(2,1)}, ...), condition=%wide.windowed_dot_general_cond_rs.3.clone, body=%wide.windowed_dot_general_body_rs.3.clone.sunk | while | flops 672382976 | bytes 20578916 | solution.py:21
  325.5 85.2 %while.14 = (bf16[1,1,2048,512]{2,3,1,0:T(8,128)(2,1)S(1)}, bf16[1,1,2048,1280]{3,2,1,0:T(8,128)(2,1)}, f32[1,32,1280]{2,1,0:T(8,128)S(1)}, f32[1,32,1280]{2,1,0...) while((bf16[1,1,2048,512]{2,3,1,0:T(8,128)(2,1)S(1)}, ...), condition=%wide.windowed_dot_general_cond_rs.2.clone, body=%wide.windowed_dot_general_body_rs.2.clone.sunk | while | flops 672382976 | bytes 21234304 | solution.py:21
  410.7 79.4 %while.13 = (bf16[1,1,2048,512]{2,3,1,0:T(8,128)(2,1)}, bf16[1,1,2048,1280]{3,2,1,0:T(8,128)(2,1)}, f32[1,32,1280]{2,1,0:T(8,128)S(1)}, f32[1,32,1280]{2,1,0:T(8...) while((bf16[1,1,2048,512]{2,3,1,0:T(8,128)(2,1)}, ...), condition=%wide.windowed_dot_general_cond_rs.1.clone, body=%wide.windowed_dot_general_body_rs.1.clone.sunk | while | flops 672382976 | bytes 21234304 | solution.py:20
  490.7 86.4 %while.12 = (bf16[1,1,2048,512]{2,3,1,0:T(8,128)(2,1)S(1)}, bf16[1,1,2048,1280]{3,2,1,0:T(8,128)(2,1)}, f32[1,32,1280]{2,1,0:T(8,128)S(1)}, f32[1,32,1280]{2,1,0...) while((bf16[1,1,2048,512]{2,3,1,0:T(8,128)(2,1)S(1)}, ...), condition=%wide.windowed_dot_general_cond_rs.clone, body=%wide.windowed_dot_general_body_rs.clone.sunk | while | flops 672382976 | bytes 21234304 | solution.py:20
  588.4 29.5 %all-reduce.10 = f32[1]{0:T(128)} all-reduce(f32[1]{0:T(128)} %bitcast.39), channel_id=13, replica_groups=mesh['rep'=4,'dp'=16] {'dp'}, use_global_device_ids=true, to_apply=%region_3.4.clone | all-reduce | flops 1 | bytes 8 | tf_op jit(solution)/vmap()/reduce_sum | solution.py:54
  625.2 32.9 %all-gather.14.cloned.1.call-done = bf16[1,2,1280,512]{3,2,1,0:T(8,128)(2,1)} async-done(((bf16[1,2,80,512]{3,2,1,0:T(8,128)(2,1)}), bf16[1,2,1280,512]{3,2,1,0:T(8,128)(2,1)}) %all-gather.14.cloned.1.call-update) | async-done | bytes 2621456 | tf_op jit(solution)/reshape | solution.py:58
  658.0 37.4 %all-gather.12.cloned.1.call-done = bf16[1,2,512,1280]{3,2,1,0:T(8,128)(2,1)} async-done(((bf16[1,2,32,1280]{3,2,1,0:T(8,128)(2,1)}), bf16[1,2,512,1280]{3,2,1,0:T(8,128)(2,1)}) %all-gather.12.cloned.1.call-update) | async-done | bytes 2621456 | tf_op jit(solution)/reshape | solution.py:58
  695.4 37.4 %all-gather.10.cloned.1.call-done = bf16[1,2,512,1280]{3,2,1,0:T(8,128)(2,1)} async-done(((bf16[1,2,32,1280]{3,2,1,0:T(8,128)(2,1)}), bf16[1,2,512,1280]{3,2,1,0:T(8,128)(2,1)}) %all-gather.10.cloned.1.call-update) | async-done | bytes 2621456 | tf_op jit(solution)/reshape | solution.py:58
  (518 shorter events, 438.2 us)
Async XLA Ops:
  7.2 650.8 %all-gather.14.cloned.1.call-start = ((), (), s32[]{:S(2)}) async-start(), calls=%async_computation.2 | async-start | bytes 2785280 | tf_op jit(solution)/reshape | solution.py:58
  86.9 9.8 %collective-permute-start.20 = (f32[1,80,512]{2,1,0:T(8,128)S(1)}, f32[1,80,512]{2,1,0:T(8,128)S(1)}, u32[]{:S(2)}, u32[]{:S(2)}) collective-permute-start(f32[1,80,512]{2,1,0:T(8,128)S(1)} %broadcast_select_fusion.34), channel_id=35, source_target_pairs={{0,1},{1,2},{2,3},{3,4},{4,5},{5,6},{6,7},{7,8},{8,9},{9,10},{10,1... | collective-permute-start | bytes 491528 | tf_op jit(solution)/vmap(transpose(jvp()))/dot_general | solution.py:9
  103.4 9.7 %collective-permute-start.20 = (f32[1,80,512]{2,1,0:T(8,128)S(1)}, f32[1,80,512]{2,1,0:T(8,128)S(1)}, u32[]{:S(2)}, u32[]{:S(2)}) collective-permute-start(f32[1,80,512]{2,1,0:T(8,128)S(1)} %broadcast_select_fusion.34), channel_id=35, source_target_pairs={{0,1},{1,2},{2,3},{3,4},{4,5},{5,6},{6,7},{7,8},{8,9},{9,10},{10,1... | collective-permute-start | bytes 491528 | tf_op jit(solution)/vmap(transpose(jvp()))/dot_general | solution.py:9
  103.5 9.6 %collective-permute-start.21 = (f32[1,80,512]{2,1,0:T(8,128)S(1)}, f32[1,80,512]{2,1,0:T(8,128)S(1)}, u32[]{:S(2)}, u32[]{:S(2)}) collective-permute-start(f32[1,80,512]{2,1,0:T(8,128)S(1)} %broadcast_select_fusion.35), channel_id=34, source_target_pairs={{0,15},{1,0},{2,1},{3,2},{4,3},{5,4},{6,5},{7,6},{8,7},{9,8},{10,9... | collective-permute-start | bytes 491528 | tf_op jit(solution)/vmap(transpose(jvp()))/dot_general | solution.py:9
  119.7 9.3 %collective-permute-start.20 = (f32[1,80,512]{2,1,0:T(8,128)S(1)}, f32[1,80,512]{2,1,0:T(8,128)S(1)}, u32[]{:S(2)}, u32[]{:S(2)}) collective-permute-start(f32[1,80,512]{2,1,0:T(8,128)S(1)} %broadcast_select_fusion.34), channel_id=35, source_target_pairs={{0,1},{1,2},{2,3},{3,4},{4,5},{5,6},{6,7},{7,8},{8,9},{9,10},{10,1... | collective-permute-start | bytes 491528 | tf_op jit(solution)/vmap(transpose(jvp()))/dot_general | solution.py:9
  135.5 9.3 %collective-permute-start.20 = (f32[1,80,512]{2,1,0:T(8,128)S(1)}, f32[1,80,512]{2,1,0:T(8,128)S(1)}, u32[]{:S(2)}, u32[]{:S(2)}) collective-permute-start(f32[1,80,512]{2,1,0:T(8,128)S(1)} %broadcast_select_fusion.34), channel_id=35, source_target_pairs={{0,1},{1,2},{2,3},{3,4},{4,5},{5,6},{6,7},{7,8},{8,9},{9,10},{10,1... | collective-permute-start | bytes 491528 | tf_op jit(solution)/vmap(transpose(jvp()))/dot_general | solution.py:9
  150.4 432.0 %collective-permute-start.29 = (f32[1,80,512]{2,1,0:T(8,128)}, f32[1,80,512]{2,1,0:T(8,128)}, u32[]{:S(2)}, u32[]{:S(2)}) collective-permute-start(f32[1,80,512]{2,1,0:T(8,128)} %get-tuple-element.47), channel_id=38, source_target_pairs={{0,1},{1,2},{2,3},{3,4},{4,5},{5,6},{6,7},{7,8},{8,9},{9,10},{10,1... | collective-permute-start | bytes 491528 | tf_op jit(solution)/vmap(transpose(jvp()))/dot_general | solution.py:9
  173.4 9.3 %collective-permute-start.16 = (f32[1,80,512]{2,1,0:T(8,128)S(1)}, f32[1,80,512]{2,1,0:T(8,128)S(1)}, u32[]{:S(2)}, u32[]{:S(2)}) collective-permute-start(f32[1,80,512]{2,1,0:T(8,128)S(1)} %broadcast_select_fusion.32), channel_id=29, source_target_pairs={{0,1},{1,2},{2,3},{3,4},{4,5},{5,6},{6,7},{7,8},{8,9},{9,10},{10,1... | collective-permute-start | bytes 491528 | tf_op jit(solution)/vmap(transpose(jvp()))/dot_general | solution.py:9
  205.0 9.3 %collective-permute-start.16 = (f32[1,80,512]{2,1,0:T(8,128)S(1)}, f32[1,80,512]{2,1,0:T(8,128)S(1)}, u32[]{:S(2)}, u32[]{:S(2)}) collective-permute-start(f32[1,80,512]{2,1,0:T(8,128)S(1)} %broadcast_select_fusion.32), channel_id=29, source_target_pairs={{0,1},{1,2},{2,3},{3,4},{4,5},{5,6},{6,7},{7,8},{8,9},{9,10},{10,1... | collective-permute-start | bytes 491528 | tf_op jit(solution)/vmap(transpose(jvp()))/dot_general | solution.py:9
  220.9 9.3 %collective-permute-start.16 = (f32[1,80,512]{2,1,0:T(8,128)S(1)}, f32[1,80,512]{2,1,0:T(8,128)S(1)}, u32[]{:S(2)}, u32[]{:S(2)}) collective-permute-start(f32[1,80,512]{2,1,0:T(8,128)S(1)} %broadcast_select_fusion.32), channel_id=29, source_target_pairs={{0,1},{1,2},{2,3},{3,4},{4,5},{5,6},{6,7},{7,8},{8,9},{9,10},{10,1... | collective-permute-start | bytes 491528 | tf_op jit(solution)/vmap(transpose(jvp()))/dot_general | solution.py:9
  235.8 347.6 %collective-permute-start.28 = (f32[1,80,512]{2,1,0:T(8,128)}, f32[1,80,512]{2,1,0:T(8,128)}, u32[]{:S(2)}, u32[]{:S(2)}) collective-permute-start(f32[1,80,512]{2,1,0:T(8,128)} %get-tuple-element.45), channel_id=32, source_target_pairs={{0,1},{1,2},{2,3},{3,4},{4,5},{5,6},{6,7},{7,8},{8,9},{9,10},{10,1... | collective-permute-start | bytes 491528 | tf_op jit(solution)/vmap(transpose(jvp()))/dot_general | solution.py:9
  254.8 10.4 %collective-permute-start.12 = (f32[1,32,1280]{2,1,0:T(8,128)S(1)}, f32[1,32,1280]{2,1,0:T(8,128)S(1)}, u32[]{:S(2)}, u32[]{:S(2)}) collective-permute-start(f32[1,32,1280]{2,1,0:T(8,128)S(1)} %broadcast_select_fusion.30), channel_id=22, source_target_pairs={{0,1},{1,2},{2,3},{3,4},{4,5},{5,6},{6,7},{7,8},{8,9},{9,10},{10,1... | collective-permute-start | bytes 491528 | tf_op jit(solution)/vmap(transpose(jvp()))/dot_general | solution.py:21
  273.6 9.2 %collective-permute-start.12 = (f32[1,32,1280]{2,1,0:T(8,128)S(1)}, f32[1,32,1280]{2,1,0:T(8,128)S(1)}, u32[]{:S(2)}, u32[]{:S(2)}) collective-permute-start(f32[1,32,1280]{2,1,0:T(8,128)S(1)} %broadcast_select_fusion.30), channel_id=22, source_target_pairs={{0,1},{1,2},{2,3},{3,4},{4,5},{5,6},{6,7},{7,8},{8,9},{9,10},{10,1... | collective-permute-start | bytes 491528 | tf_op jit(solution)/vmap(transpose(jvp()))/dot_general | solution.py:21
  325.5 253.1 %collective-permute-start.27 = (f32[1,32,1280]{2,1,0:T(8,128)}, f32[1,32,1280]{2,1,0:T(8,128)}, u32[]{:S(2)}, u32[]{:S(2)}) collective-permute-start(f32[1,32,1280]{2,1,0:T(8,128)} %get-tuple-element.43), channel_id=25, source_target_pairs={{0,1},{1,2},{2,3},{3,4},{4,5},{5,6},{6,7},{7,8},{8,9},{9,10},{10,1... | collective-permute-start | bytes 491528 | tf_op jit(solution)/vmap(transpose(jvp()))/dot_general | solution.py:21
  326.2 9.4 %collective-permute-start.8 = (f32[1,32,1280]{2,1,0:T(8,128)}, f32[1,32,1280]{2,1,0:T(8,128)}, u32[]{:S(2)}, u32[]{:S(2)}) collective-permute-start(f32[1,32,1280]{2,1,0:T(8,128)} %broadcast_select_fusion.28), channel_id=16, source_target_pairs={{0,1},{1,2},{2,3},{3,4},{4,5},{5,6},{6,7},{7,8},{8,9},{9,10},{10,1... | collective-permute-start | bytes 491528 | tf_op jit(solution)/vmap(transpose(jvp()))/dot_general | solution.py:21
  347.7 9.4 %collective-permute-start.8 = (f32[1,32,1280]{2,1,0:T(8,128)}, f32[1,32,1280]{2,1,0:T(8,128)}, u32[]{:S(2)}, u32[]{:S(2)}) collective-permute-start(f32[1,32,1280]{2,1,0:T(8,128)} %broadcast_select_fusion.28), channel_id=16, source_target_pairs={{0,1},{1,2},{2,3},{3,4},{4,5},{5,6},{6,7},{7,8},{8,9},{9,10},{10,1... | collective-permute-start | bytes 491528 | tf_op jit(solution)/vmap(transpose(jvp()))/dot_general | solution.py:21
  369.2 9.4 %collective-permute-start.8 = (f32[1,32,1280]{2,1,0:T(8,128)}, f32[1,32,1280]{2,1,0:T(8,128)}, u32[]{:S(2)}, u32[]{:S(2)}) collective-permute-start(f32[1,32,1280]{2,1,0:T(8,128)} %broadcast_select_fusion.28), channel_id=16, source_target_pairs={{0,1},{1,2},{2,3},{3,4},{4,5},{5,6},{6,7},{7,8},{8,9},{9,10},{10,1... | collective-permute-start | bytes 491528 | tf_op jit(solution)/vmap(transpose(jvp()))/dot_general | solution.py:21
  390.7 9.4 %collective-permute-start.8 = (f32[1,32,1280]{2,1,0:T(8,128)}, f32[1,32,1280]{2,1,0:T(8,128)}, u32[]{:S(2)}, u32[]{:S(2)}) collective-permute-start(f32[1,32,1280]{2,1,0:T(8,128)} %broadcast_select_fusion.28), channel_id=16, source_target_pairs={{0,1},{1,2},{2,3},{3,4},{4,5},{5,6},{6,7},{7,8},{8,9},{9,10},{10,1... | collective-permute-start | bytes 491528 | tf_op jit(solution)/vmap(transpose(jvp()))/dot_general | solution.py:21
  491.7 9.7 %collective-permute-start = (f32[1,32,1280]{2,1,0:T(8,128)}, f32[1,32,1280]{2,1,0:T(8,128)}, u32[]{:S(2)}, u32[]{:S(2)}) collective-permute-start(f32[1,32,1280]{2,1,0:T(8,128)} %broadcast_select_fusion.24), channel_id=3, source_target_pairs={{0,1},{1,2},{2,3},{3,4},{4,5},{5,6},{6,7},{7,8},{8,9},{9,10},{10,1... | collective-permute-start | bytes 491528 | tf_op jit(solution)/vmap(transpose(jvp()))/dot_general | solution.py:20
  513.4 9.7 %collective-permute-start = (f32[1,32,1280]{2,1,0:T(8,128)}, f32[1,32,1280]{2,1,0:T(8,128)}, u32[]{:S(2)}, u32[]{:S(2)}) collective-permute-start(f32[1,32,1280]{2,1,0:T(8,128)} %broadcast_select_fusion.24), channel_id=3, source_target_pairs={{0,1},{1,2},{2,3},{3,4},{4,5},{5,6},{6,7},{7,8},{8,9},{9,10},{10,1... | collective-permute-start | bytes 491528 | tf_op jit(solution)/vmap(transpose(jvp()))/dot_general | solution.py:20
  535.2 9.7 %collective-permute-start = (f32[1,32,1280]{2,1,0:T(8,128)}, f32[1,32,1280]{2,1,0:T(8,128)}, u32[]{:S(2)}, u32[]{:S(2)}) collective-permute-start(f32[1,32,1280]{2,1,0:T(8,128)} %broadcast_select_fusion.24), channel_id=3, source_target_pairs={{0,1},{1,2},{2,3},{3,4},{4,5},{5,6},{6,7},{7,8},{8,9},{9,10},{10,1... | collective-permute-start | bytes 491528 | tf_op jit(solution)/vmap(transpose(jvp()))/dot_general | solution.py:20
  557.0 9.7 %collective-permute-start = (f32[1,32,1280]{2,1,0:T(8,128)}, f32[1,32,1280]{2,1,0:T(8,128)}, u32[]{:S(2)}, u32[]{:S(2)}) collective-permute-start(f32[1,32,1280]{2,1,0:T(8,128)} %broadcast_select_fusion.24), channel_id=3, source_target_pairs={{0,1},{1,2},{2,3},{3,4},{4,5},{5,6},{6,7},{7,8},{8,9},{9,10},{10,1... | collective-permute-start | bytes 491528 | tf_op jit(solution)/vmap(transpose(jvp()))/dot_general | solution.py:20
  620.9 74.6 %all-gather.12.cloned.1.call-start = ((), (), s32[]{:S(2)}) async-start(), calls=%async_computation.1 | async-start | bytes 2785280 | tf_op jit(solution)/reshape | solution.py:58
  623.0 109.8 %all-gather.10.cloned.1.call-start = ((), (), s32[]{:S(2)}) async-start(), calls=%async_computation | async-start | bytes 2785280 | tf_op jit(solution)/reshape | solution.py:58
  (132 other events, 1035.5 us)
Sparse Core Ops, SparseCore 0:
  621.0 37.0 all-gather.13
  660.3 35.0 all-gather.11
  697.6 35.0 all-gather.9
where the time goes:
time: 758 us; the launch traced here: 746 us
  matrix products  205 us (27%)
  starting transfers between devices  157 us (21%)
  waiting for transfers between devices  121 us (16%)
  other arithmetic  105 us (14%)
  local copies, waits for them, and re-layouts  63.7 us (8%)
  loops' own time  47.9 us (6%)
  blocking collectives  29.5 us (4%)
  between operations  17.8 us (2%)
    reshape x3, waiting for transfers between devices, step(): t.reshape(-1, *t.shape[2:])  108 us
    dot_general x19, matrix products, layer(): gate = jnp.dot(a, w['w_gate'], preferred_element_type=jnp.float32)  76.3 us
    dot_general x19, matrix products, layer(): up = jnp.dot(a, w['w_up'], preferred_element_type=jnp.float32)  76 us
    dot_general x34, starting transfers between devices, matmul(): jnp.dot(a, w, preferred_element_type=jnp.float32).astype(jnp.bfloat16)  59.7 us
    dot_general x19, matrix products, matmul(): jnp.dot(a, w, preferred_element_type=jnp.float32).astype(jnp.bfloat16)  52.6 us
    dot_general x34, starting transfers between devices, layer(): up = jnp.dot(a, w['w_up'], preferred_element_type=jnp.float32)  49 us
    dot_general x34, starting transfers between devices, layer(): gate = jnp.dot(a, w['w_gate'], preferred_element_type=jnp.float32)  47.6 us
    unnamed x55, local copies, waits for them, and re-layouts  41.1 us
  transfers between devices with their start and end apart: 105, of which 21 were waited for; matrix products, arithmetic and copies ran while one was open for 36% of the time, Pallas kernels for 0%

commit v1 on v0

v1 whole, which is shorter than its diff:
```python
import functools

import jax
import jax.numpy as jnp
from jax import lax
from jax.experimental import pallas as pl
from jax.experimental.pallas import tpu as pltpu
from jax.sharding import PartitionSpec as P

MESH = pl.DeviceIdType.MESH
F32, BF16 = jnp.float32, jnp.bfloat16


def dot(a, b, ca, cb):
    return lax.dot_general(a, b, (((ca,), (cb,)), ((), ())), preferred_element_type=F32)


def scale_of(wide):
    return lax.rsqrt(jnp.mean(wide * wide, -1, keepdims=True) + 1e-6)


def normed(h):
    wide = h.astype(F32)
    return (wide * scale_of(wide)).astype(BF16)


def sigmoid(t):
    return 0.5 * jnp.tanh(0.5 * t) + 0.5


def rounded(t):
    return t.astype(BF16).astype(F32)


def kernel(n, tile, *refs):
    ins, outs, rest = refs[:11], refs[11:22], refs[22:]
    x_in, dy_in, *w_in = ins[:5]
    m_in, v_in = ins[5:8], ins[8:11]
    w_out, m_out, v_out = outs[0:3], outs[3:6], outs[6:9]
    kept_gate, kept_up = outs[9:11]
    h_ref, dh_ref, a_refs, w_refs = rest[0], rest[1], rest[2:4], rest[4:7]
    u_ref, dg_ref, du_ref, gate_ref, up_ref = rest[7:12]
    m_refs, v_refs = rest[12:15], rest[15:18]
    kinds = {"wide": rest[18:24], "tall": rest[24:30]}
    norms = rest[30]
    (load_sem, keep_sem, swap_s, swap_r, ring_s, ring_r, norm_s, norm_r, own_s, state_s, ag_s, ag_r, mate_s, mate_r, out_s) = rest[31:]

    tokens, d = h_ref.shape
    ff = u_ref.shape[1]
    half_way = n // 4
    me = lax.axis_index("dp")
    chip, core = me // 2, lax.rem(me, 2)
    chips = n // 2
    mate = me + 1 - 2 * core
    ahead = (lax.rem(me + 2, n), lax.rem(me + n - 2, n))

    def remote(src, dst, send, recv, to):
        return pltpu.make_async_remote_copy(
            src_ref=src, dst_ref=dst, send_sem=send, recv_sem=recv, device_id={"dp": to}, device_id_type=MESH
        )

    barrier = pltpu.get_barrier_semaphore()
    for k in range(1, n):
        pl.semaphore_signal(barrier, inc=1, device_id={"dp": lax.rem(me + k, n)}, device_id_type=MESH)

    loads = []

    def load(src, dst):
        copy = pltpu.make_async_copy(src, dst, load_sem.at[len(loads)])
        copy.start()
        loads.append(copy)
        return copy

    for src, dst in ((x_in.at[0], h_ref), (w_in[0].at[0], w_refs[0].at[0]), (w_in[1].at[0], w_refs[1].at[0]), (w_in[2].at[0], w_refs[2].at[0])):
        load(src, dst)
    for which in range(3):
        load(w_in[which].at[1], w_refs[which].at[1])
    load(dy_in.at[0], dh_ref)
    n_first = len(loads)
    for which in range(3):
        load(m_in[which], m_refs[which])
        load(v_in[which], v_refs[which])
    for copy in loads[:n_first]:
        copy.wait()

    wg, wu, wd = w_refs
    cuts = (slice(0, 2 * ff // 5), slice(2 * ff // 5, ff))

    def keep(rows):
        return (
            pltpu.make_async_copy(gate_ref, kept_gate.at[rows, :], keep_sem.at[0]),
            pltpu.make_async_copy(up_ref, kept_up.at[rows, :], keep_sem.at[1]),
        )

    def rows_of(t, size):
        return pl.ds(pl.multiple_of(t * size, size), size)

    def forward(t, _):
        rows = rows_of(t, tile)

        @pl.when(t > 0)
        def _():
            for copy in keep(rows_of(t - 1, tile)):
                copy.wait()

        x = h_ref[rows, :]
        a = normed(x)
        a_refs[0][rows, :] = a
        for cut in cuts:
            gate, up = dot(a, wg[0, :, cut], 1, 0), dot(a, wu[0, :, cut], 1, 0)
            gate_ref[:, cut] = gate
            up_ref[:, cut] = up
            u_ref[rows, cut] = (gate * sigmoid(gate) * up).astype(BF16)
        for copy in keep(rows):
            copy.start()
        h = (x.astype(F32) + rounded(dot(u_ref[rows, :], wd[0], 1, 0))).astype(BF16)
        h_ref[rows, :] = h
        a = normed(h)
        a_refs[1][rows, :] = a
        by_y = dh_ref[rows, :]
        for cut in cuts:
            gate, up = dot(a, wg[1, :, cut], 1, 0), dot(a, wu[1, :, cut], 1, 0)
            through(rows, cut, gate, up, rounded(dot(by_y, wd[1, cut, :], 1, 1)))
        return 0

    def through(rows, cut, gate, up, by_u):
        sig = sigmoid(gate)
        silu = gate * sig
        u_ref[rows, cut] = (silu * up).astype(BF16)
        du_ref[rows, cut] = (by_u * silu).astype(BF16)
        dg_ref[rows, cut] = (by_u * up * (sig + silu * (1.0 - sig))).astype(BF16)

    tiles = tokens // tile
    lax.fori_loop(0, tiles, forward, 0)
    for copy in keep(rows_of(tiles - 1, tile)):
        copy.wait()

    part = tile // 2

    def bring(t, side):
        rows = pl.ds(pl.multiple_of(t * tile + side * part, part), part)
        here = pl.ds(side * part, part)
        return (
            pltpu.make_async_copy(kept_gate.at[rows, :], gate_ref.at[here, :], keep_sem.at[2 + side]),
            pltpu.make_async_copy(kept_up.at[rows, :], up_ref.at[here, :], keep_sem.at[4 + side]),
        )

    for side in range(2):
        for copy in bring(0, side):
            copy.start()

    def into_norm(t, _):
        rows = rows_of(t, tile)
        by_a = rounded(rounded(dot(dg_ref[rows, :], wg[1], 1, 1)) + rounded(dot(du_ref[rows, :], wu[1], 1, 1)))
        wide = h_ref[rows, :].astype(F32)
        scale = scale_of(wide)
        unit = wide * scale
        by_h = scale * (by_a - unit * jnp.mean(by_a * unit, -1, keepdims=True))
        dh_ref[rows, :] = (dh_ref[rows, :].astype(F32) + rounded(by_h)).astype(BF16)
        return 0

    def into_hidden(t, _):
        by_u = rounded(dot(dh_ref[rows_of(t, tile), :], wd[0], 1, 1))
        for side in range(2):
            for copy in bring(t, side):
                copy.wait()
            here = slice(side * part, (side + 1) * part)
            rows = pl.ds(pl.multiple_of(t * tile + side * part, part), part)
            through(rows, slice(None), gate_ref[here, :], up_ref[here, :], by_u[here])

        @pl.when(t + 1 < tiles)
        def _():
            for side in range(2):
                for copy in bring(t + 1, side):
                    copy.start()

        return 0

    sent = []
    pending = {}

    def of(kind, slot):
        total, _, back, ring, first, result = kinds[kind]
        return total.at[slot], None, back.at[slot], ring.at[slot], first.at[slot], result.at[slot]

    def swap(number, kind, slot, left, right, cuts):
        total, _, back, *_ = of(kind, slot)
        out = kinds[kind][1].at[slot // 2 if kind == "wide" else 0]
        rows = total.shape[1]
        if number >= 3:
            pending[number - 3][2].wait_send()
        for first, last in zip(cuts[:-1], cuts[1:], strict=True):
            pairs = dot(left[...], right[:, first:last], 0, 0).reshape(chips, 2, rows, last - first)
            low, high = pairs[:, 0], pairs[:, 1]
            total[:, :, first:last] = jnp.where(core == 0, low, high)
            out[:, :, first:last] = jnp.where(core == 0, high, low).astype(BF16)
        copy = remote(out, back, swap_s.at[number], swap_r.at[number], mate)
        copy.start()
        if number >= 3:
            sent.append(copy)
        pending[number] = (kind, slot, copy)

    def halves(columns):
        return slice(0, columns // 2), slice(columns // 2, columns)

    def hop(number, way, step, src, dst):
        return remote(src, dst, ring_s.at[number, way, step], ring_r.at[number, way, step], ahead[way])

    def block_at(step, way):
        return lax.rem(chip + half_way - 1 - step + chips, chips) if way == 0 else lax.rem(chip - half_way + 1 + step + chips, chips)

    def arriving(number, way, step, kind, slot):
        _, _, _, ring, first, _ = of(kind, slot)
        columns = ring.shape[3]
        if step:
            return hop(number, way, step, ring.at[way, step - 1], ring.at[way, step])
        side = pl.ds(0, columns // 2) if way == 0 else pl.ds(columns // 2, columns // 2)
        return hop(number, way, 0, first.at[way], ring.at[way, 0, :, side])

    def send(number, step, kind, slot):
        for way in range(2):
            copy = arriving(number, way, step, kind, slot)
            copy.start()
            sent.append(copy)

    def advance(number, stage):
        kind, slot, copy = pending[number]
        total, _, back, ring, first, result = of(kind, slot)
        sides = halves(total.shape[2])
        if stage == 0:
            copy.wait_recv()
            total[...] += back[...].astype(F32)
            far = total[lax.rem(chip + half_way, chips)]
            for way in range(2):
                first[way] = far[:, sides[way]].astype(BF16)
            send(number, 0, kind, slot)
            return
        for way in range(2):
            arriving(number, way, stage - 1, kind, slot).wait_recv()
            if stage < half_way:
                own = total[block_at(stage - 1, way)]
                if stage == 1:
                    ring[way, 0, :, sides[way]] = (own[:, sides[way]] + ring[way, 0, :, sides[way]].astype(F32)).astype(BF16)
                    ring[way, 0, :, sides[1 - way]] = own[:, sides[1 - way]].astype(BF16)
                else:
                    ring[way, stage - 1] = (own + ring[way, stage - 1].astype(F32)).astype(BF16)
        if stage < half_way:
            send(number, stage, kind, slot)
            return
        grad = rounded(total[chip] + ring[0, half_way - 1].astype(F32) + ring[1, half_way - 1].astype(F32))
        result[...] = grad
        squares = jnp.sum((grad * grad).reshape(-1, 8, grad.shape[1]), 0)
        squares = sum(squares[:, i : i + 128] for i in range(0, squares.shape[1], 128))
        norms[me] = squares if number == 0 else norms[me] + squares

    def by_down(number, slot):
        swap(number, "tall", slot, u_ref, dh_ref, (0, d // 2, d))

    def by_wide(number, slot, a, hidden):
        swap(number, "wide", slot, a, hidden, (0, 3 * ff // 5, ff))

    pl.semaphore_wait(barrier, n - 1)
    by_down(0, 1)
    by_wide(1, 1, a_refs[1], dg_ref)
    advance(0, 0)
    by_wide(2, 3, a_refs[1], du_ref)
    advance(0, 1)
    advance(1, 0)
    lax.fori_loop(0, tiles // 2, into_norm, 0)
    advance(0, 2)
    advance(1, 1)
    advance(2, 0)
    lax.fori_loop(tiles // 2, tiles, into_norm, 0)
    advance(0, 3)
    advance(1, 2)
    advance(2, 1)
    lax.fori_loop(0, tiles // 2, into_hidden, 0)
    advance(0, 4)
    advance(1, 3)
    advance(2, 2)
    lax.fori_loop(tiles // 2, tiles, into_hidden, 0)
    by_down(3, 0)
    advance(1, 4)
    advance(2, 3)
    by_wide(4, 0, a_refs[0], dg_ref)
    advance(3, 0)
    advance(2, 4)
    by_wide(5, 2, a_refs[0], du_ref)
    for now in range(7):
        for number in (3, 4, 5):
            stage = now + 4 - number
            if (number, stage) != (3, 0) and 0 <= stage <= half_way:
                advance(number, stage)

    count = sum(w.size for w in w_refs)
    for k in range(1, n):
        copy = remote(norms.at[me], norms.at[me], norm_s.at[k], norm_r.at[k], lax.rem(me + k, n))
        copy.start()
        sent.append(copy)
    for copy in loads[n_first:]:
        copy.wait()
    for k in range(1, n):
        other = lax.rem(me + n - k, n)
        remote(norms.at[other], norms.at[other], norm_s.at[k], norm_r.at[k], other).wait_recv()
    squares = jnp.sum(jnp.sum(jnp.sum(norms[...], 0), 1, keepdims=True), 0, keepdims=True)
    factor = jnp.minimum(1.0, 0.5 * lax.rsqrt(squares / count + 1e-30))

    local = []

    def start(copy, to):
        copy.start()
        to.append(copy)

    def piece(ref, which, layer, device, side=None):
        rows = ref.shape[1] // n
        at = ref.at[layer, pl.ds(pl.multiple_of(device * rows, rows), rows)]
        if side is None:
            return at
        columns = ref.shape[2] // 2
        return ref.at[layer, pl.ds(pl.multiple_of(device * rows, rows), rows), pl.ds(side * columns, columns)]

    order = [(layer, which) for layer in (1, 0) for which in (2, 0, 1)]
    slots = {(1, 2): ("tall", 1), (1, 0): ("wide", 1), (1, 1): ("wide", 3), (0, 2): ("tall", 0), (0, 0): ("wide", 0), (0, 1): ("wide", 2)}

    def to_mate(i, layer, which, place, device, side=None):
        return remote(
            piece(w_refs[which], which, layer, device, side), piece(w_out[which], which, layer, device, side),
            mate_s.at[i, place], mate_r.at[i, place], mate,
        )

    def to_out(i, layer, which, place, device, side=None):
        return pltpu.make_async_copy(
            piece(w_refs[which], which, layer, device, side), piece(w_out[which], which, layer, device, side), out_s.at[i, place]
        )

    def along(i, layer, which, way, step, device, side=None):
        at = piece(w_refs[which], which, layer, device, side)
        return remote(at, at, ag_s.at[i, way, step], ag_r.at[i, way, step], ahead[way])

    for i, (layer, which) in enumerate(order):
        kind, slot = slots[layer, which]
        g = of(kind, slot)[5][...] * factor
        m = 0.9 * m_refs[which][layer] + 0.1 * g
        v = 0.95 * v_refs[which][layer] + 0.05 * g * g
        m_refs[which][layer] = m
        v_refs[which][layer] = v
        rows = w_refs[which].shape[1] // n
        mine = pl.ds(pl.multiple_of(me * rows, rows), rows)
        w = w_refs[which][layer, mine, :].astype(F32)
        w_refs[which][layer, mine, :] = (w - 0.02 * (m * lax.rsqrt(v + 1e-8) + 0.1 * w)).astype(BF16)
        for way in range(2):
            start(along(i, layer, which, way, 0, me), sent)
        start(to_mate(i, layer, which, 0, me), sent)
        start(to_out(i, layer, which, 0, me), local)
        start(pltpu.make_async_copy(m_refs[which].at[layer], m_out[which].at[layer], state_s.at[0, i]), local)
        start(pltpu.make_async_copy(v_refs[which].at[layer], v_out[which].at[layer], state_s.at[1, i]), local)

    def origin(way, hops):
        return lax.rem(me + 2 * (n - hops), n) if way == 0 else lax.rem(me + 2 * hops, n)

    for hops in range(1, half_way + 1):
        for i, (layer, which) in enumerate(order):
            for way in range(2):
                device = origin(way, hops)
                side = way if hops == half_way else None
                along(i, layer, which, way, hops - 1, device, side).wait_recv()
                if hops < half_way:
                    start(along(i, layer, which, way, hops, device, way if hops == half_way - 1 else None), sent)
                place = 2 * hops - 1 + way
                start(to_mate(i, layer, which, place, device, side), sent)
                start(to_out(i, layer, which, place, device, side), local)

    for i, (layer, which) in enumerate(order):
        to_mate(i, layer, which, 0, mate).wait_recv()
        for hops in range(1, half_way + 1):
            for way in range(2):
                device = lax.rem(mate + 2 * (n - hops), n) if way == 0 else lax.rem(mate + 2 * hops, n)
                to_mate(i, layer, which, 2 * hops - 1 + way, device, way if hops == half_way else None).wait_recv()
    for copy in local:
        copy.wait()
    for copy in sent:
        copy.wait_send()


def solution(mesh):
    n = mesh.shape["dp"]

    def step(*args):
        x, w_gate, w_down = args[0], args[2], args[4]
        _, tokens, d = x.shape
        layers, _, ff = w_gate.shape
        chips, way = n // 2, n // 4
        tile = tokens // 4
        weights, moments = args[2:5], args[5:11]
        vmem, dma = pltpu.VMEM, pltpu.SemaphoreType.DMA

        def ring_buffers(slots, rows, columns):
            return [
                vmem((slots, chips, rows, columns), F32),
                vmem((slots // layers, chips, rows, columns), BF16),
                vmem((slots, chips, rows, columns), BF16),
                vmem((slots, 2, way, rows, columns), BF16),
                vmem((slots, 2, rows, columns // 2), BF16),
                vmem((slots, rows, columns), F32),
            ]

        scratch = [
            *(vmem((tokens, d), BF16) for _ in range(4)),
            *(vmem(w.shape, BF16) for w in weights),
            *(vmem((tokens, ff), BF16) for _ in range(3)),
            *(vmem((tile, ff), F32) for _ in range(2)),
            *(vmem(t.shape, F32) for t in moments),
            *ring_buffers(2 * layers, d // n, ff),
            *ring_buffers(layers, ff // n, d),
            vmem((n, 8, 128), F32),
            dma((14,)), dma((6,)), dma((6,)), dma((6,)), dma((6, 2, way)), dma((6, 2, way)), dma((n,)), dma((n,)),
            dma((6,)), dma((2, 6)), dma((6, 2, way)), dma((6, 2, way)), dma((6, 2 * way + 1)), dma((6, 2 * way + 1)), dma((6, 2 * way + 1)),
        ]
        shapes = [jax.ShapeDtypeStruct(w.shape, BF16) for w in weights] + [jax.ShapeDtypeStruct(t.shape, F32) for t in moments]
        shapes += [jax.ShapeDtypeStruct((tokens, ff), F32)] * 2
        anywhere = pl.BlockSpec(memory_space=pl.ANY)
        out = pl.pallas_call(
            functools.partial(kernel, n, tile),
            out_shape=shapes,
            in_specs=[anywhere] * len(args),
            out_specs=[anywhere] * len(shapes),
            scratch_shapes=scratch,
            compiler_params=pltpu.CompilerParams(collective_id=0, has_side_effects=True, vmem_limit_bytes=67_043_328),
            name="train_step",
        )(*args)
        return tuple(out[:9])

    whole, rows = P(None, None, None), P(None, "dp", None)
    return jax.shard_map(
        step,
        mesh=mesh,
        in_specs=(P(("rep", "dp"), None, None),) * 2 + (whole,) * 3 + (rows,) * 6,
        out_specs=(P("rep", None, None),) * 3 + (P("rep", "dp", None),) * 6,
        check_vma=False,
    )
```

time: 758 us -> 165 us (0.22); the launches traced: 746 us -> 165 us
  matrix products: 205 us -> 0 us
  starting transfers between devices: 157 us -> 0 us
  Pallas kernels: 0 us -> 153 us
  waiting for transfers between devices: 121 us -> 0 us
  other arithmetic: 105 us -> 0 us
  local copies, waits for them, and re-layouts: 63.7 us -> 12.1 us
  loops' own time: 47.9 us -> 0 us
  blocking collectives: 29.5 us -> 0 us
  between operations: 17.8 us -> 0.68 us
    dot_general x57 -> x0, matrix products: 205 us -> none  [the longest x19 76.3 us: layer(): gate = jnp.dot(a, w['w_gate'], preferred_element_type=jnp.float32)]
    dot_general x102 -> x0, starting transfers between devices: 156 us -> none  [the longest x34 59.7 us: matmul(): jnp.dot(a, w, preferred_element_type=jnp.float32).astype(jnp.bfloat16)]
    pallas_call x0 -> x1, Pallas kernels: none -> 153 us  [step(): pl.pallas_call(functools.partial(kernel, n, tile), out_shape=shapes, in_s...]
    reshape x3 -> x0, waiting for transfers between devices: 108 us -> none  [step(): t.reshape(-1, *t.shape[2:])]
    dot_general x96 -> x0, other arithmetic: 74.3 us -> none
    another operation x6 -> x0, loops' own time: 47.9 us -> none  [the longest x2 16.4 us: layer(): gate = jnp.dot(a, w['w_gate'], preferred_element_type=jnp.float32)]
    reduce_sum x1 -> x0, blocking collectives: 29.5 us -> none  [of_a_group(): jnp.sum(g * g)]
    unnamed x55 -> x25, local copies, waits for them, and re-layouts: 41.1 us -> 12.1 us
  transfers between devices with their start and end apart: 105 -> 0, of which waited for: 21 -> 0; matrix products, arithmetic and copies ran while one was open for 36% -> 0% of each run, Pallas kernels for 0% -> 0%
where the time goes in v1:
time: 165 us
  Pallas kernels  153 us (93%)
  local copies, waits for them, and re-layouts  12.1 us (7%)
    pallas_call x1, Pallas kernels, step(): pl.pallas_call(functools.partial(kernel, n, tile), out_shape=shapes, in_s...  153 us
    unnamed x25, local copies, waits for them, and re-layouts  12.1 us

profile of v1, /device:TPU:21, one launch (start us, length us, event | category | flops | bytes accessed | tf_op | source)
XLA Modules:
  0.0 165.4 jit_solution(7772065045172993876)
XLA Ops:
  0.6 152.6 %train_step.1 = (bf16[2,512,1280]{2,1,0:T(8,128)(2,1)}, bf16[2,512,1280]{2,1,0:T(8,128)(2,1)}, bf16[2,1280,512]{2,1,0:T(8,128)(2,1)}, f32[2,32,1280]{2,1,0:T(8,1...) custom-call(bf16[1,2048,512]{2,1,0:T(8,128)(2,1)} %refs_0_.1, ...), custom_call_target="tpu_custom_call" | custom-call | tf_op jit(solution)/shard_map/train_step/pallas_call | solution.py:422
  153.2 0.0 copy-start.1
  153.2 3.6 %copy.29 = bf16[2,512,1280]{2,1,0:T(8,128)(2,1)} copy(bf16[2,512,1280]{2,1,0:T(8,128)(2,1)} %get-tuple-element.36) | data formatting | bytes 5242880
  156.8 0.0 copy-done.1
  156.8 0.0 copy-start
  156.8 1.5 copy.30
  158.3 1.2 copy-done
  159.5 0.0 copy-start.7
  159.5 0.0 copy-start.6
  159.5 0.0 copy-start.5
  159.5 0.0 copy-start.4
  159.5 1.5 copy.31
  161.0 0.0 copy-done.7
  161.0 0.7 copy.32
  161.7 0.0 copy-done.6
  161.7 0.7 copy.33
  162.5 0.0 copy-done.5
  162.5 0.7 copy.34
  163.2 0.0 copy-done.4
  163.2 0.7 copy.35
  163.9 0.0 copy-done.3
  163.9 0.7 copy.36
  164.6 0.0 copy-done.2
  164.6 0.7 copy.37
  (2 shorter events, 0.0 us)
Async XLA Ops:
  153.2 3.6 %copy-start.1 = (bf16[2,512,1280]{2,1,0:T(8,128)(2,1)S(1)}, bf16[2,512,1280]{2,1,0:T(8,128)(2,1)}, u32[]{:S(2)}) copy-start(bf16[2,512,1280]{2,1,0:T(8,128)(2,1)} %get-tuple-element.37) | copy-start | bytes 7864324
  156.8 2.7 %copy-start = (bf16[2,1280,512]{2,1,0:T(8,128)(2,1)S(1)}, bf16[2,1280,512]{2,1,0:T(8,128)(2,1)}, u32[]{:S(2)}) copy-start(bf16[2,1280,512]{2,1,0:T(8,128)(2,1)} %get-tuple-element.38) | copy-start | bytes 7864324
  159.5 1.5 copy-start.7
  159.5 2.2 %copy-start.6 = (f32[2,32,1280]{2,1,0:T(8,128)S(1)}, f32[2,32,1280]{2,1,0:T(8,128)}, u32[]{:S(2)}) copy-start(f32[2,32,1280]{2,1,0:T(8,128)} %get-tuple-element.40) | copy-start | bytes 983044
  159.5 3.0 %copy-start.5 = (f32[2,80,512]{2,1,0:T(8,128)S(1)}, f32[2,80,512]{2,1,0:T(8,128)}, u32[]{:S(2)}) copy-start(f32[2,80,512]{2,1,0:T(8,128)} %get-tuple-element.41) | copy-start | bytes 983044
  159.5 3.7 %copy-start.4 = (f32[2,32,1280]{2,1,0:T(8,128)S(1)}, f32[2,32,1280]{2,1,0:T(8,128)}, u32[]{:S(2)}) copy-start(f32[2,32,1280]{2,1,0:T(8,128)} %get-tuple-element.42) | copy-start | bytes 983044
  161.0 2.9 %copy-start.3 = (f32[2,32,1280]{2,1,0:T(8,128)S(1)}, f32[2,32,1280]{2,1,0:T(8,128)}, u32[]{:S(2)}) copy-start(f32[2,32,1280]{2,1,0:T(8,128)} %get-tuple-element.43) | copy-start | bytes 983044
  161.0 3.6 %copy-start.2 = (f32[2,80,512]{2,1,0:T(8,128)S(1)}, f32[2,80,512]{2,1,0:T(8,128)}, u32[]{:S(2)}) copy-start(f32[2,80,512]{2,1,0:T(8,128)} %get-tuple-element.44) | copy-start | bytes 983044
